TPU v7x, 32 devices: a whole 2x2x4 slice. The times are simulated.
32 devices in a mesh: rows: 8 (over z, y), cols: 4 (over x, core).
Axes of the slice: x: 2, y: 2, z: 4, core: 2. Of those that a mesh axis runs over, the one named last changes fastest.
Arguments:
- factor_a: bfloat16 [16384, 48, 48], P('rows'), may hold values from -0.875 to 0.875
- factor_b: bfloat16 [16384, 48, 48], P('rows'), may hold values from -0.046875 to 0.046875
- next_factor: bfloat16 [16384, 48, 48], P(('rows', 'cols')), may hold values from -6 to 6
- sketch_leg: bfloat16 [48, 32], replicated, may hold values from -6 to 6
- sketch_rows: bfloat16 [16384, 32], P('rows', 'cols'), may hold values from -6 to 6
Outputs:
- basis: float32 [32, 16384, 48], P(None, ('rows', 'cols'))
- squeezed: float32 [32, 48], replicated
All inputs are finite; a program needn't handle non-finite values.
Results may differ from a plain program's by a relative error of at most 0.0003.
Values sent between devices are 32-bit elements; how exact they have to be, the bound alone decides.
No kernel may reach another device: no remote copies, remote signals or barrier semaphores. Data moves between devices by JAX's collectives and lax.ppermute only.
A program may use at most 128 MiB of HBM per device.

v0:
```python
import jax
import jax.numpy as jnp
from jax import lax
from jax.sharding import PartitionSpec as P


def per_device(factor_a, factor_b, next_factor, sketch_leg, sketch_rows):
    high = lax.Precision.HIGHEST
    local_rows = factor_a.shape[0]
    width = factor_a.shape[1]
    col_parts = lax.axis_size("cols")
    quarter = local_rows // col_parts
    col_index = lax.axis_index("cols")
    count = local_rows * lax.axis_size("rows") * width
    start = col_index * quarter
    far_part = jnp.einsum("sp,syk->pyk", sketch_rows, factor_b, preferred_element_type=jnp.float32)
    far = lax.psum(far_part, "rows")
    far_all = lax.all_gather(far, "cols", axis=0, tiled=True)
    own_rows = lax.dynamic_slice_in_dim(factor_a, start, quarter, 0)
    near = jnp.einsum("sxk,xp->psk", own_rows, sketch_leg, preferred_element_type=jnp.float32)
    sketch = jnp.einsum("psk,pyk->psy", near, far_all, precision=high)
    columns = sketch.shape[0]
    flat = sketch.reshape(columns, quarter * width)
    own_next = next_factor.reshape(quarter * width, width).astype(jnp.float32)
    gram_part = jnp.dot(flat, flat.T, precision=high)
    root_count = jnp.sqrt(jnp.float32(count))
    gram = lax.psum(gram_part, ("rows", "cols")) / count
    lower = jnp.linalg.cholesky(gram)
    basis = jax.scipy.linalg.solve_triangular(lower, flat, lower=True)
    squeeze_part = jnp.dot(basis, own_next, precision=high)
    squeezed = lax.psum(squeeze_part, ("rows", "cols")) / root_count
    return (basis.reshape(columns, quarter, width), squeezed)


def solution(mesh):
    return jax.shard_map(
        per_device,
        mesh=mesh,
        in_specs=(
            P("rows", None, None),
            P("rows", None, None),
            P(("rows", "cols"), None, None),
            P(),
            P("rows", "cols"),
        ),
        out_specs=(P(None, ("rows", "cols"), None), P()),
        check_vma=False,
    )
```

profile of v0, /device:TPU:0, one launch (start us, length us, event | category | flops | bytes accessed | tf_op | source)
XLA Modules:
  0.0 238.8 jit_solution(5856863479625042245)
XLA Ops:
  7.2 0.0 copy-start
  7.2 0.0 all-reduce.2.cloned.1.call-start
  7.2 0.7 copy-done
  7.9 8.9 %fusion.12 = f32[8,48,48]{2,0,1:T(8,128)} fusion(bf16[2048,48,48]{0,2,1:T(8,128)(2,1)} %param.6, bf16[2048,8]{0,1:T(8,128)(2,1)S(1)} %copy-done), kind=kOutput, calls=%fused_computation.8 | convolution fusion | flops 75497472 | bytes 9543680 | tf_op jit(solution)/shard_map/sp,syk->pyk/dot_general | solution.py:16
  16.8 0.0 copy-start.2
  16.8 0.0 all-reduce.2.cloned.1.call-update
  16.9 1.8 constant_dynamic-slice_fusion
  18.7 0.0 copy-done.2
  18.7 0.0 copy-start.1
  18.7 3.4 %fusion.6 = f32[32,512,48]{1,0,2:T(8,128)} fusion(bf16[512,48,48]{0,2,1:T(8,128)(2,1)S(1)} %constant_dynamic-slice_fusion, bf16[48,32]{0,1:T(8,128)(2,1)S(1)} %copy-done.2), kind=kOutput, calls=%fused_computation.6 | convolution fusion | flops 75497472 | bytes 5508096 | tf_op jit(solution)/shard_map/sxk,xp->psk/dot_general | solution.py:20
  22.1 0.0 copy-done.1
  22.1 5.0 %copy.27 = bf16[512,48,48]{1,0,2:T(8,128)(2,1)} copy(bf16[512,48,48]{0,2,1:T(8,128)(2,1)S(1)} %copy-done.1) | data formatting | bytes 4718592 | tf_op args[2]
  27.2 14.0 %reshape.25 = bf16[24576,48]{0,1:T(8,128)(2,1)} reshape(bf16[512,48,48]{1,0,2:T(8,128)(2,1)} %copy.27) | data formatting | bytes 4718592 | tf_op jit(solution)/shard_map/reshape | solution.py:24
  41.1 49.3 %all-reduce.2.cloned.1.call-done = f32[8,48,48]{2,0,1:T(8,128)} async-done(((f32[8,48,48]{2,0,1:T(8,128)}), f32[8,48,48]{2,0,1:T(8,128)}) %all-reduce.2.cloned.1.call-update) | async-done | bytes 73744 | tf_op jit(solution)/shard_map/psum | solution.py:17
  90.4 1.0 copy.20
  91.4 8.8 %all_gather.3 = f32[32,48,48]{2,1,0:T(8,128)S(1)} all-gather(f32[8,48,48]{2,1,0:T(8,128)S(1)} %copy.20), channel_id=1, replica_groups=mesh['rows'=8,'cols'=4] {'cols'}, dimensions={0}, use_global_device_ids=true | all-gather | bytes 368640 | tf_op jit(solution)/shard_map/all_gather | solution.py:18
  100.1 6.7 %fusion.2 = f32[32,512,48]{1,2,0:T(8,128)S(1)} fusion(f32[32,48,48]{2,1,0:T(8,128)S(1)} %all_gather.3, f32[32,512,48]{1,0,2:T(8,128)} %fusion.6), kind=kOutput, calls=%fused_computation.2 | convolution fusion | flops 452984832 | bytes 6586368 | tf_op jit(solution)/shard_map/psk,pyk->psy/dot_general | solution.py:21
  106.9 4.2 %fusion.9 = f32[32,32]{0,1:T(8,128)S(1)} fusion(f32[32,512,48]{1,2,0:T(8,128)S(1)} %fusion.2), kind=kOutput, calls=%fused_computation.7 | convolution fusion | flops 301989888 | bytes 3149824 | tf_op jit(solution)/shard_map/dot_general | solution.py:25
  111.1 4.7 %copy.26 = f32[32,512,48]{2,1,0:T(8,128)} copy(f32[32,512,48]{1,2,0:T(8,128)S(1)} %fusion.2) | data formatting | bytes 6291456 | tf_op jit(solution)/shard_map/psk,pyk->psy/dot_general | solution.py:21
  115.8 38.7 %psum.22 = f32[32,32]{0,1:T(8,128)S(1)} all-reduce(f32[32,32]{0,1:T(8,128)S(1)} %fusion.9), channel_id=1, replica_groups=mesh['rows'=8,'cols'=4] {'rows','cols'}, use_global_device_ids=true, to_apply=%region_1.0 | all-reduce | flops 1024 | bytes 8192 | tf_op jit(solution)/shard_map/psum | solution.py:27
  154.5 0.1 copy.25
  154.5 2.9 %cholesky.16 = f32[32,32]{1,0:T(8,128)S(1)} custom-call(f32[32,32]{1,0:T(8,128)S(1)} %fusion.17), custom_call_target="Cholesky" | custom-call | tf_op jit(solution)/shard_map/jit(cholesky)/cholesky | solution.py:28
  157.5 0.6 compare_reduce_fusion
  158.1 0.7 fusion.14
  158.8 2.4 %custom-call.7 = f32[1,32,32]{1,2,0:T(8,128)S(1)} custom-call(f32[1,32,32]{2,1,0:T(8,128)S(1)} %fusion.14), custom_call_target="InvertDiagBlocksLowerTriangular" | custom-call | tf_op jit(solution)/shard_map/jit(_solve_triangular)/triangular_solve | solution.py:29
  161.2 9.8 %reshape.23 = f32[32,24576]{1,0:T(8,128)} reshape(f32[32,512,48]{2,1,0:T(8,128)} %copy.26) | data formatting | bytes 6291456 | tf_op jit(solution)/shard_map/reshape | solution.py:23
  171.0 4.6 %fusion.15 = f32[32,24576]{1,0:T(8,128)S(1)} fusion(f32[32,24576]{1,0:T(8,128)} %reshape.23, f32[1,32,32]{1,2,0:T(8,128)S(1)} %custom-call.7), kind=kOutput, calls=%fused_computation.12 | convolution fusion | flops 301989888 | bytes 6295552 | tf_op jit(solution)/shard_map/jit(_solve_triangular)/triangular_solve | solution.py:29
  175.6 5.4 %reshape.24 = f32[32,512,48]{2,1,0:T(8,128)} reshape(f32[32,24576]{1,0:T(8,128)S(1)} %fusion.15) | data formatting | bytes 6291456 | tf_op jit(solution)/shard_map/reshape | solution.py:32
  181.0 3.7 %fusion.19 = f32[32,48]{1,0:T(8,128)S(1)} fusion(f32[32,24576]{1,0:T(8,128)S(1)} %fusion.15, bf16[24576,48]{0,1:T(8,128)(2,1)} %reshape.25), kind=kOutput, calls=%fused_computation.24 | convolution fusion | flops 452984832 | bytes 5511168 | tf_op jit(solution)/shard_map/dot_general | solution.py:30
  184.7 40.1 %psum.23 = f32[32,48]{1,0:T(8,128)S(1)} all-reduce(f32[32,48]{1,0:T(8,128)S(1)} %fusion.19), channel_id=1, replica_groups=mesh['rows'=8,'cols'=4] {'rows','cols'}, use_global_device_ids=true, to_apply=%region_4.5 | all-reduce | flops 1536 | bytes 12288 | tf_op jit(solution)/shard_map/psum | solution.py:31
  224.8 0.6 broadcast_multiply_fusion
  225.5 6.5 %copy.28 = f32[32,512,48]{1,2,0:T(8,128)} copy(f32[32,512,48]{2,1,0:T(8,128)} %reshape.24) | data formatting | bytes 6291456
  (3 shorter events, 0.0 us)
Async XLA Ops:
  7.2 0.8 copy-start
  7.2 83.2 %all-reduce.2.cloned.1.call-start = ((), (), s32[]{:S(2)}) async-start(), calls=%async_computation | async-start | bytes 393216 | tf_op jit(solution)/shard_map/psum | solution.py:17
  16.8 1.9 copy-start.2
  18.7 3.4 %copy-start.1 = (bf16[512,48,48]{0,2,1:T(8,128)(2,1)S(1)}, bf16[512,48,48]{0,2,1:T(8,128)(2,1)}, u32[]{:S(2)}) copy-start(bf16[512,48,48]{0,2,1:T(8,128)(2,1)} %param.7) | copy-start | bytes 7077892
Sparse Core Ops, SparseCore 0:
  17.0 73.3 all-reduce.1
where the time goes:
time: 239 us
  blocking collectives  87.6 us (37%)
  waiting for transfers between devices  49.3 us (21%)
  local copies, waits for them, and re-layouts  48.9 us (20%)
  matrix products  31.5 us (13%)
  between operations  14.1 us (6%)
  other arithmetic  7.3 us (3%)
    psum x1, waiting for transfers between devices, per_device(): far = lax.psum(far_part, 'rows')  49.3 us
    psum x1, blocking collectives, per_device(): squeezed = lax.psum(squeeze_part, ('rows', 'cols')) / root_count  40.1 us
    psum x1, blocking collectives, per_device(): gram = lax.psum(gram_part, ('rows', 'cols')) / count  38.7 us
    reshape x1, local copies, waits for them, and re-layouts, per_device(): own_next = next_factor.reshape(quarter * width, width).astype(jnp.float32)  14 us
    unnamed x8, local copies, waits for them, and re-layouts  12.3 us
    reshape x1, local copies, waits for them, and re-layouts, per_device(): flat = sketch.reshape(columns, quarter * width)  9.77 us
    dot_general x1, matrix products, per_device(): jnp.einsum('sp,syk->pyk', sketch_rows, factor_b, preferred_element_type=j...  8.91 us
    all_gather x1, blocking collectives, per_device(): far_all = lax.all_gather(far, 'cols', axis=0, tiled=True)  8.76 us
  transfers between devices with their start and end apart: 1, of which 1 were waited for; matrix products, arithmetic and copies ran while one was open for 10% of the time, Pallas kernels for 0%

commit v1 on v0

--- a/solution.py
+++ b/solution.py
@@ -2,6 +2,15 @@
 import jax.numpy as jnp
 from jax import lax
 from jax.sharding import PartitionSpec as P
+
+
+def doubling_sum(x, axis):
+    size = lax.axis_size(axis)
+    acc, stride = (x, 1)
+    while stride < size:
+        acc = acc + lax.ppermute(acc, axis, [(i, i ^ stride) for i in range(size)])
+        stride = 2 * stride
+    return acc
 
 
 def per_device(factor_a, factor_b, next_factor, sketch_leg, sketch_rows):
@@ -14,7 +23,7 @@
     count = local_rows * lax.axis_size("rows") * width
     start = col_index * quarter
     far_part = jnp.einsum("sp,syk->pyk", sketch_rows, factor_b, preferred_element_type=jnp.float32)
-    far = lax.psum(far_part, "rows")
+    far = doubling_sum(far_part, "rows")
     far_all = lax.all_gather(far, "cols", axis=0, tiled=True)
     own_rows = lax.dynamic_slice_in_dim(factor_a, start, quarter, 0)
     near = jnp.einsum("sxk,xp->psk", own_rows, sketch_leg, preferred_element_type=jnp.float32)

time: 239 us -> 190 us (0.79)
  waiting for transfers between devices: 49.3 us -> 7.33 us
  between operations: 14.1 us -> 0.72 us
  starting transfers between devices: 0.04 us -> 7.47 us
    psum x1 -> x0, waiting for transfers between devices: 49.3 us -> none  [per_device(): far = lax.psum(far_part, 'rows')]
    ppermute x0 -> x3, starting transfers between devices: none -> 7.47 us  [doubling_sum(): acc = acc + lax.ppermute(acc, axis, [(i, i ^ stride) for i in range(size)])]
    ppermute x0 -> x3, waiting for transfers between devices: none -> 7.33 us  [doubling_sum(): acc = acc + lax.ppermute(acc, axis, [(i, i ^ stride) for i in range(size)])]
    unnamed x8 -> x10, local copies, waits for them, and re-layouts: 12.3 us -> 12.3 us
  transfers between devices with their start and end apart: 1 -> 3, of which waited for: 1 -> 2; matrix products, arithmetic and copies ran while one was open for 10% -> 13% of each run, Pallas kernels for 0% -> 0%
where the time goes in v1:
time: 190 us; the launch traced here: 189 us
  blocking collectives  88.3 us (46%)
  local copies, waits for them, and re-layouts  48 us (25%)
  matrix products  29.7 us (16%)
  starting transfers between devices  7.47 us (4%)
  other arithmetic  7.36 us (4%)
  waiting for transfers between devices  7.33 us (4%)
    psum x1, blocking collectives, per_device(): squeezed = lax.psum(squeeze_part, ('rows', 'cols')) / root_count  40 us
    psum x1, blocking collectives, per_device(): gram = lax.psum(gram_part, ('rows', 'cols')) / count  39.5 us
    reshape x1, local copies, waits for them, and re-layouts, per_device(): own_next = next_factor.reshape(quarter * width, width).astype(jnp.float32)  14 us
    unnamed x10, local copies, waits for them, and re-layouts  12.3 us
    reshape x1, local copies, waits for them, and re-layouts, per_device(): flat = sketch.reshape(columns, quarter * width)  9.77 us
    all_gather x1, blocking collectives, per_device(): far_all = lax.all_gather(far, 'cols', axis=0, tiled=True)  8.78 us
    ppermute x3, starting transfers between devices, doubling_sum(): acc = acc + lax.ppermute(acc, axis, [(i, i ^ stride) for i in range(size)])  7.47 us
    ppermute x3, waiting for transfers between devices, doubling_sum(): acc = acc + lax.ppermute(acc, axis, [(i, i ^ stride) for i in range(size)])  7.33 us
  transfers between devices with their start and end apart: 3, of which 2 were waited for; matrix products, arithmetic and copies ran while one was open for 13% of the time, Pallas kernels for 0%

profile of v1, /device:TPU:0, one launch (start us, length us, event | category | flops | bytes accessed | tf_op | source)
XLA Modules:
  0.0 188.9 jit_solution(4254687292305546478)
XLA Ops:
  0.6 0.0 copy-start
  0.6 0.7 copy-done
  1.4 7.0 %fusion.11 = f32[8,48,48]{2,0,1:T(8,128)S(1)} fusion(bf16[2048,48,48]{0,2,1:T(8,128)(2,1)} %param.6, bf16[2048,8]{0,1:T(8,128)(2,1)S(1)} %copy-done), kind=kOutput, calls=%fused_computation.9 | convolution fusion | flops 75497472 | bytes 9543680 | tf_op jit(solution)/shard_map/sp,syk->pyk/dot_general | solution.py:25
  8.4 0.0 copy-start.3
  8.4 3.0 %collective-permute-start = (f32[8,48,48]{2,0,1:T(8,128)S(1)}, f32[8,48,48]{2,0,1:T(8,128)S(1)}, u32[]{:S(2)}, u32[]{:S(2)}) collective-permute-start(f32[8,48,48]{2,0,1:T(8,128)S(1)} %fusion.11), channel_id=1, source_target_pairs={{0,4},{4,0},{8,12},{12,8},{16,20},{20,16},{24,28},{28,24},{1,5},{5... | collective-permute-start | bytes 221192 | tf_op jit(solution)/shard_map/ppermute | solution.py:11
  11.4 4.9 %collective-permute-done = f32[8,48,48]{2,0,1:T(8,128)S(1)} collective-permute-done((f32[8,48,48]{2,0,1:T(8,128)S(1)}, f32[8,48,48]{2,0,1:T(8,128)S(1)}, u32[]{:S(2)}, u32[]{:S(2)}) %collective-permute-start) | collective-permute-done | bytes 73760 | tf_op jit(solution)/shard_map/ppermute | solution.py:11
  16.3 1.9 collective-permute-start.1
  18.2 1.8 constant_dynamic-slice_fusion
  20.0 0.0 copy-start.2
  20.0 2.4 %collective-permute-done.1 = f32[8,48,48]{2,0,1:T(8,128)S(1)} collective-permute-done((f32[8,48,48]{2,0,1:T(8,128)S(1)}, f32[8,48,48]{2,0,1:T(8,128)S(1)}, u32[]{:S(2)}, u32[]{:S(2)}) %collective-permute-start.1) | collective-permute-done | bytes 73760 | tf_op jit(solution)/shard_map/ppermute | solution.py:11
  22.5 2.6 %collective-permute-start.2 = (f32[8,48,48]{2,0,1:T(8,128)S(1)}, f32[8,48,48]{2,0,1:T(8,128)S(1)}, u32[]{:S(2)}, u32[]{:S(2)}) collective-permute-start(f32[8,48,48]{2,0,1:T(8,128)S(1)} %add.30), channel_id=1, source_target_pairs={{0,16},{4,20},{8,24},{12,28},{16,0},{20,4},{24,8},{28,12},{1,17},{... | collective-permute-start | bytes 221192 | tf_op jit(solution)/shard_map/ppermute | solution.py:11
  25.1 0.0 copy-done.3
  25.1 3.4 %fusion.5 = f32[512,48,32]{0,2,1:T(8,128)} fusion(bf16[512,48,48]{0,2,1:T(8,128)(2,1)S(1)} %constant_dynamic-slice_fusion, bf16[48,32]{0,1:T(8,128)(2,1)S(1)} %copy-done.3), kind=kOutput, calls=%fused_computation.5 | convolution fusion | flops 75497472 | bytes 5508096 | tf_op jit(solution)/shard_map/sxk,xp->psk/dot_general | solution.py:29
  28.5 0.0 copy-done.2
  28.5 5.0 %copy.19 = bf16[512,48,48]{1,0,2:T(8,128)(2,1)} copy(bf16[512,48,48]{0,2,1:T(8,128)(2,1)S(1)} %copy-done.2) | data formatting | bytes 4718592 | tf_op args[2]
  33.5 14.0 %reshape.25 = bf16[24576,48]{0,1:T(8,128)(2,1)} reshape(bf16[512,48,48]{1,0,2:T(8,128)(2,1)} %copy.19) | data formatting | bytes 4718592 | tf_op jit(solution)/shard_map/reshape | solution.py:33
  47.5 0.0 collective-permute-done.2
  47.5 8.8 %all_gather.3 = f32[32,48,48]{2,0,1:T(8,128)S(1)} all-gather(f32[8,48,48]{2,0,1:T(8,128)S(1)} %add.31), channel_id=1, replica_groups=mesh['rows'=8,'cols'=4] {'cols'}, dimensions={0}, use_global_device_ids=true | all-gather | bytes 368640 | tf_op jit(solution)/shard_map/all_gather | solution.py:27
  56.3 6.8 %fusion = f32[32,512,48]{1,2,0:T(8,128)S(1)} fusion(f32[512,48,32]{0,2,1:T(8,128)} %fusion.5, f32[32,48,48]{2,0,1:T(8,128)S(1)} %all_gather.3), kind=kOutput, calls=%fused_computation | convolution fusion | flops 452984832 | bytes 6586368 | tf_op jit(solution)/shard_map/psk,pyk->psy/dot_general | solution.py:30
  63.1 4.2 %fusion.7 = f32[32,32]{0,1:T(8,128)S(1)} fusion(f32[32,512,48]{1,2,0:T(8,128)S(1)} %fusion), kind=kOutput, calls=%fused_computation.7 | convolution fusion | flops 301989888 | bytes 3149824 | tf_op jit(solution)/shard_map/dot_general | solution.py:34
  67.3 4.7 %copy.18 = f32[32,512,48]{2,1,0:T(8,128)} copy(f32[32,512,48]{1,2,0:T(8,128)S(1)} %fusion) | data formatting | bytes 6291456 | tf_op jit(solution)/shard_map/psk,pyk->psy/dot_general | solution.py:30
  72.0 39.5 %psum.14 = f32[32,32]{0,1:T(8,128)S(1)} all-reduce(f32[32,32]{0,1:T(8,128)S(1)} %fusion.7), channel_id=1, replica_groups=mesh['rows'=8,'cols'=4] {'rows','cols'}, use_global_device_ids=true, to_apply=%region_0.0 | all-reduce | flops 1024 | bytes 8192 | tf_op jit(solution)/shard_map/psum | solution.py:36
  111.5 0.1 copy.17
  111.6 2.9 %cholesky.16 = f32[32,32]{1,0:T(8,128)S(1)} custom-call(f32[32,32]{1,0:T(8,128)S(1)} %fusion.16), custom_call_target="Cholesky" | custom-call | tf_op jit(solution)/shard_map/jit(cholesky)/cholesky | solution.py:37
  114.6 0.6 compare_reduce_fusion
  115.2 0.7 fusion.13
  115.9 2.4 %custom-call.7 = f32[1,32,32]{1,2,0:T(8,128)S(1)} custom-call(f32[1,32,32]{2,1,0:T(8,128)S(1)} %fusion.13), custom_call_target="InvertDiagBlocksLowerTriangular" | custom-call | tf_op jit(solution)/shard_map/jit(_solve_triangular)/triangular_solve | solution.py:38
  118.3 9.8 %reshape.23 = f32[32,24576]{1,0:T(8,128)} reshape(f32[32,512,48]{2,1,0:T(8,128)} %copy.18) | data formatting | bytes 6291456 | tf_op jit(solution)/shard_map/reshape | solution.py:32
  128.1 4.6 %fusion.14 = f32[32,24576]{1,0:T(8,128)S(1)} fusion(f32[32,24576]{1,0:T(8,128)} %reshape.23, f32[1,32,32]{1,2,0:T(8,128)S(1)} %custom-call.7), kind=kOutput, calls=%fused_computation.13 | convolution fusion | flops 301989888 | bytes 6295552 | tf_op jit(solution)/shard_map/jit(_solve_triangular)/triangular_solve | solution.py:38
  132.7 5.4 %reshape.24 = f32[32,512,48]{2,1,0:T(8,128)} reshape(f32[32,24576]{1,0:T(8,128)S(1)} %fusion.14) | data formatting | bytes 6291456 | tf_op jit(solution)/shard_map/reshape | solution.py:41
  138.1 3.7 %fusion.18 = f32[32,48]{1,0:T(8,128)S(1)} fusion(f32[32,24576]{1,0:T(8,128)S(1)} %fusion.14, bf16[24576,48]{0,1:T(8,128)(2,1)} %reshape.25), kind=kOutput, calls=%fused_computation.25 | convolution fusion | flops 452984832 | bytes 5511168 | tf_op jit(solution)/shard_map/dot_general | solution.py:39
  141.8 40.0 %psum.15 = f32[32,48]{1,0:T(8,128)S(1)} all-reduce(f32[32,48]{1,0:T(8,128)S(1)} %fusion.18), channel_id=1, replica_groups=mesh['rows'=8,'cols'=4] {'rows','cols'}, use_global_device_ids=true, to_apply=%region_3.4 | all-reduce | flops 1536 | bytes 12288 | tf_op jit(solution)/shard_map/psum | solution.py:40
  181.8 0.0 copy-start.1
  181.8 0.6 broadcast_multiply_fusion
  182.4 6.5 %copy.20 = f32[32,512,48]{1,2,0:T(8,128)} copy(f32[32,512,48]{2,1,0:T(8,128)} %reshape.24) | data formatting | bytes 6291456
  188.9 0.0 copy-done.1
  (6 shorter events, 0.1 us)
Async XLA Ops:
  0.6 0.8 copy-start
  8.4 16.7 %copy-start.3 = (bf16[48,32]{0,1:T(8,128)(2,1)S(1)}, bf16[48,32]{0,1:T(8,128)(2,1)}, u32[]{:S(2)}) copy-start(bf16[48,32]{0,1:T(8,128)(2,1)} %param.8) | copy-start | bytes 9220
  8.4 7.9 %collective-permute-start = (f32[8,48,48]{2,0,1:T(8,128)S(1)}, f32[8,48,48]{2,0,1:T(8,128)S(1)}, u32[]{:S(2)}, u32[]{:S(2)}) collective-permute-start(f32[8,48,48]{2,0,1:T(8,128)S(1)} %fusion.11), channel_id=1, source_target_pairs={{0,4},{4,0},{8,12},{12,8},{16,20},{20,16},{24,28},{28,24},{1,5},{5... | collective-permute-start | bytes 221192 | tf_op jit(solution)/shard_map/ppermute | solution.py:11
  16.3 6.1 %collective-permute-start.1 = (f32[8,48,48]{2,0,1:T(8,128)S(1)}, f32[8,48,48]{2,0,1:T(8,128)S(1)}, u32[]{:S(2)}, u32[]{:S(2)}) collective-permute-start(f32[8,48,48]{2,0,1:T(8,128)S(1)} %add.29), channel_id=1, source_target_pairs={{0,8},{4,12},{8,0},{12,4},{16,24},{20,28},{24,16},{28,20},{1,9},{5... | collective-permute-start | bytes 221192 | tf_op jit(solution)/shard_map/ppermute | solution.py:11
  20.0 8.5 %copy-start.2 = (bf16[512,48,48]{0,2,1:T(8,128)(2,1)S(1)}, bf16[512,48,48]{0,2,1:T(8,128)(2,1)}, u32[]{:S(2)}) copy-start(bf16[512,48,48]{0,2,1:T(8,128)(2,1)} %param.7) | copy-start | bytes 7077892
  22.5 25.0 %collective-permute-start.2 = (f32[8,48,48]{2,0,1:T(8,128)S(1)}, f32[8,48,48]{2,0,1:T(8,128)S(1)}, u32[]{:S(2)}, u32[]{:S(2)}) collective-permute-start(f32[8,48,48]{2,0,1:T(8,128)S(1)} %add.30), channel_id=1, source_target_pairs={{0,16},{4,20},{8,24},{12,28},{16,0},{20,4},{24,8},{28,12},{1,17},{... | collective-permute-start | bytes 221192 | tf_op jit(solution)/shard_map/ppermute | solution.py:11
  181.8 7.1 %copy-start.1 = (bf16[2048,8]{0,1:T(8,128)(2,1)S(1)}, bf16[2048,8]{0,1:T(8,128)(2,1)}, u32[]{:S(2)}) copy-start(bf16[2048,8]{0,1:T(8,128)(2,1)} %param.9) | copy-start | bytes 98308
